TPU v7x, 32 devices: a whole 2x2x4 slice. The times are simulated.
32 devices in a mesh: rows: 16 (over z, x, core), cols: 2 (over y).
Axes of the slice: x: 2, y: 2, z: 4, core: 2. Of those that a mesh axis runs over, the one named last changes fastest.
Arguments:
- image: float32 [1024, 16384], P('rows', 'cols'), may hold values from -6 to 6
- cloud_mask: int32 [1024, 16384], P('rows', 'cols'), may hold values 0 or 1
- tile_weight: int32 [128, 128], P('rows', 'cols'), may hold values from 1 to 8
- owner: int32 [128], replicated, may hold values from 0 to 15, as said below
Outputs:
- solution: float32 [1024, 16384], P('rows', 'cols')
- objective: float32 [3], replicated
Inputs may be any that keep to these rules, and one draw needn't show every extreme that they name: `owner`: every index of rows owns exactly 8 blocks, and the 8 blocks b*8 to b*8 + 7 have 8 different owners for every b.
All inputs are finite; a program needn't handle non-finite values. No bound on the sum of `cloud_mask` on one device may be relied on, other than what follows from the above.
Results may differ from a plain program's by a relative error of at most 0.0001.
Values sent between devices are 32-bit elements; how exact they have to be, the bound alone decides.
A program may use at most 64 MiB of HBM per device.

v0:
```python
import jax
import jax.numpy as jnp
from jax import lax
from jax.sharding import PartitionSpec as P

BR = 8
TW = 128
ITERS = 3


fidelity_scale = 0.25
tau_step = 0.35
sigma_step = 0.35
tv_weight = 0.3


def passed_along(block, axis, distance):
    devices = range(lax.axis_size(axis))
    route = [(i - distance, i) for i in devices if i - distance in devices]
    return lax.ppermute(block, axis, route)


def per_device(image, cloud_mask, tile_weight, owner):
    rows_here, width_here = image.shape
    blocks_here = rows_here // BR
    row_count = lax.axis_size("rows")
    col_count = lax.axis_size("cols")
    own_row = lax.axis_index("rows")
    own_col = lax.axis_index("cols")
    total_blocks = owner.shape[0]
    height_all = total_blocks * BR
    width_all = width_here * col_count
    pixel_total = height_all * width_all
    tile_count = width_here // TW
    clear_sky = (1 - cloud_mask).astype(jnp.float32).reshape(blocks_here, BR, tile_count, TW)
    fidelity = (
        fidelity_scale * tile_weight.astype(jnp.float32)[:, None, :, None] * clear_sky
    ).reshape(rows_here, width_here)
    local_index = jnp.arange(blocks_here, dtype=jnp.int32)
    home_blocks = own_row * blocks_here + local_index
    targets = owner[home_blocks]
    owned = jnp.argsort((owner != own_row).astype(jnp.int32), stable=True)[:blocks_here]
    senders = owned // blocks_here
    last_column = ((jnp.arange(width_here) == width_here - 1) & (own_col == col_count - 1))[None, :]
    has_next = (home_blocks + 1 < total_blocks)[:, None]
    has_prev = (home_blocks > 0)[:, None]
    primal = image
    extrap = image
    dual_rows = jnp.zeros_like(image)
    dual_cols = jnp.zeros_like(image)
    values = []
    for step in range(ITERS):
        shaped = extrap.reshape(blocks_here, BR, width_here)
        first_rows = shaped[:, 0, :]
        below_arriving = passed_along(first_rows[:1], "rows", -1)
        follow = jnp.concatenate([first_rows[1:], below_arriving], axis=0)
        bottom = jnp.where(has_next, follow - shaped[:, -1, :], 0.0)
        grad_r = jnp.concatenate(
            [shaped[:, 1:, :] - shaped[:, :-1, :], bottom[:, None, :]], axis=1
        ).reshape(rows_here, width_here)
        right_edge = passed_along(extrap[:, 0][None, :], "cols", -1)
        grad_c = jnp.concatenate(
            [extrap[:, 1:] - extrap[:, :-1], right_edge[0][:, None] - extrap[:, -1:]], axis=1
        )
        grad_c = jnp.where(last_column, 0.0, grad_c)
        trial_rows = dual_rows + sigma_step * grad_r
        trial_cols = dual_cols + sigma_step * grad_c
        shrink = jnp.maximum(
            1.0, jnp.sqrt(trial_rows * trial_rows + trial_cols * trial_cols) / tv_weight
        )
        dual_rows = trial_rows / shrink
        dual_cols = trial_cols / shrink
        dual_shaped = dual_rows.reshape(blocks_here, BR, width_here)
        last_rows = dual_shaped[:, -1, :]
        arriving = passed_along(last_rows[-1:], "rows", 1)
        leading = jnp.where(has_prev, jnp.concatenate([arriving, last_rows[:-1]], axis=0), 0.0)
        earlier_rows = jnp.concatenate([leading[:, None, :], dual_shaped[:, :-1, :]], axis=1)
        div_rows = (dual_shaped - earlier_rows).reshape(rows_here, width_here)
        left_edge = passed_along(dual_cols[:, -1][None, :], "cols", 1)
        div_cols = dual_cols - jnp.concatenate([left_edge[0][:, None], dual_cols[:, :-1]], axis=1)
        updated = (primal + tau_step * (div_rows + div_cols) + tau_step * fidelity * image) / (
            1.0 + tau_step * fidelity
        )
        misfit = updated - image
        partial_sum = jnp.sum(0.5 * fidelity * misfit * misfit) + tv_weight * jnp.sum(
            jnp.sqrt(grad_r * grad_r + grad_c * grad_c)
        )
        values.append(lax.psum(partial_sum, ("rows", "cols")) / pixel_total)
        extrap = 2.0 * updated - primal
        primal = updated
    primal, values = (primal, values)
    empty = jnp.zeros((row_count, BR, width_here), jnp.float32)
    solution = lax.all_to_all(
        empty.at[targets].set(primal.reshape(blocks_here, BR, width_here)),
        "rows",
        split_axis=0,
        concat_axis=0,
        tiled=True,
    )[senders].reshape(rows_here, width_here)
    objective = jnp.stack(values)
    return (solution, objective)


def solution(mesh):
    in_specs = (P("rows", "cols"), P("rows", "cols"), P("rows", "cols"), P())
    out_specs = (P("rows", "cols"), P())
    return jax.shard_map(
        per_device, mesh=mesh, in_specs=in_specs, out_specs=out_specs, check_vma=False
    )
```

profile of v0, /device:TPU:27, one launch (start us, length us, event | category | flops | bytes accessed | tf_op | source)
XLA Modules:
  0.0 260.1 jit_solution(12863689969462286870)
XLA Ops:
  0.6 1.0 slice_bitcast_fusion.5
  1.6 2.6 collective-permute-start
  4.2 0.9 slice_reduce_fusion.5
  5.1 1.3 collective-permute-start.1
  6.4 3.9 %slice_subtract_fusion.4 = f32[8,7,8192]{2,1,0:T(8,128)} fusion(f32[8,8,8192]{2,1,0:T(8,128)} %bitcast.143), kind=kLoop, calls=%fused_computation.14 | loop fusion | flops 458752 | bytes 5505024 | tf_op jit(solution)/shard_map/sub | solution.py:59
  10.3 2.0 fusion.46
  12.3 1.9 slice_subtract_fusion.5
  14.2 1.7 broadcast_bitcast_fusion
  16.7 3.9 %fusion.34 = f32[8,8,8192]{2,1,0:T(8,128)S(1)} fusion(f32[8,8,1]{2,1,0:T(8,128)S(1)} %bitcast.162, f32[8,8,8191]{2,1,0:T(8,128)} %fusion.46, pred[8192]{0:T(1024)(128)(4,1)S(1)} %fusion.36, f32[8,1,8192]{2,1,0:T(1,128)S(1)} %broadcast_select_fusion.5, f32[8,7,8192]{2,1,0:T(8,128)} %slice_subtract_fusion.4), kind=kLoop, calls=%fused_computation.76 | loop fusion | flops 5767168 | bytes 6299648 | tf_op jit(solution)/shard_map/div | solution.py:71
  20.7 1.3 collective-permute-start.2
  22.0 1.5 fusion.35
  23.6 1.3 copy-done.9
  25.1 4.0 %collective-permute-start.3 = (f32[1,64]{1,0:T(1,128)S(1)}, f32[1,64]{1,0:T(1,128)S(1)}, u32[]{:S(2)}, u32[]{:S(2)}) collective-permute-start(f32[1,64]{1,0:T(1,128)S(1)} %bitcast.185), channel_id=1, source_target_pairs={{0,1},{2,3},{4,5},{6,7},{8,9},{10,11},{12,13},{14,15},{16,17},{18,... | collective-permute-start | bytes 776 | tf_op jit(solution)/shard_map/ppermute | solution.py:20
  30.2 9.5 %multiply_subtract_fusion.1 = (f32[64,8192]{1,0:T(8,128)S(1)}, f32[64,8192]{1,0:T(8,128)}, f32[64,8192]{1,0:T(8,128)}, f32[64,8192]{1,0:T(8,128)}) fusion(f32[64,8192]{1,0:T(8,128)S(1)} %copy-done.1, f32[64,8192]{1,0:T(8,128)} %copy-done.9, f32[64,8191]{1,0:T(8,128)} %bitcast.155, f32[64,1]{1,0:T(8,128)S(1)} %copy.32, f32[8,7,8192]{2,1,0:T(8,128)} %bitcast.156, ...), kind=kLoop, calls=%fused_computation.74 | loop fusion | flops 14680064 | bytes 25174016 | tf_op jit(solution)/shard_map/sub | solution.py:89
  39.8 2.0 fusion.45
  41.9 2.0 slice_subtract_fusion.2
  43.9 1.3 collective-permute-start.5
  45.1 1.5 slice_subtract_fusion.3
  46.8 4.1 %collective-permute-start.4 = (f32[1,8192]{1,0:T(1,128)S(1)}, f32[1,8192]{1,0:T(1,128)S(1)}, u32[]{:S(2)}, u32[]{:S(2)}) collective-permute-start(f32[1,8192]{1,0:T(1,128)S(1)} %slice_bitcast_fusion.3), channel_id=1, source_target_pairs={{2,0},{4,2},{6,4},{8,6},{10,8},{12,10},{14,12},{16,14},{18,16},{20... | collective-permute-start | bytes 98312 | tf_op jit(solution)/shard_map/ppermute | solution.py:20
  51.0 0.8 slice_subtract_fusion.10
  51.9 2.1 broadcast_select_fusion.4
  54.0 7.7 %fusion.31 = (f32[8,8,8192]{2,1,0:T(8,128)S(1)}, f32[8,8,8192]{2,1,0:T(8,128)}) fusion(f32[8,8,8192]{2,1,0:T(8,128)} %copy-done.12, f32[8,1,8192]{2,1,0:T(1,128)S(1)} %broadcast_select_fusion.4, f32[8,7,8192]{2,1,0:T(8,128)} %slice_subtract_fusion.3, f32[8,8,1]{2,1,0:T(8,128)S(1)} %bitcast.165, f32[8,8,8191]{2,1,0:T(8,128)} %fusion.45, ...), kind=kLoop, calls=%fused_computation.70 | loop fusion | flops 12582912 | bytes 14688256 | tf_op jit(solution)/shard_map/div | solution.py:71
  61.7 1.3 collective-permute-start.6
  63.1 1.7 fusion.32
  64.8 1.3 copy-done.7
  66.3 4.3 %collective-permute-start.7 = (f32[1,64]{1,0:T(1,128)S(1)}, f32[1,64]{1,0:T(1,128)S(1)}, u32[]{:S(2)}, u32[]{:S(2)}) collective-permute-start(f32[1,64]{1,0:T(1,128)S(1)} %bitcast.182), channel_id=1, source_target_pairs={{0,1},{2,3},{4,5},{6,7},{8,9},{10,11},{12,13},{14,15},{16,17},{18,... | collective-permute-start | bytes 776 | tf_op jit(solution)/shard_map/ppermute | solution.py:20
  70.6 0.6 gather_fusion
  71.2 1.7 slice.244
  73.4 9.8 %multiply_subtract_fusion = (f32[64,8192]{1,0:T(8,128)S(1)}, f32[64,8192]{1,0:T(8,128)}, f32[64,8192]{1,0:T(8,128)}) fusion(f32[64,8192]{1,0:T(8,128)} %get-tuple-element.20, f32[64,8192]{1,0:T(8,128)S(1)} %copy-done.1, f32[64,8192]{1,0:T(8,128)} %get-tuple-element.21, f32[64,8192]{1,0:T(8,128)} %copy-done.7, f32[64,8191]{1,0:T(8,128)} %bitcast.154, ...), kind=kLoop, calls=%fused_computation.67 | loop fusion | flops 14155776 | bytes 27271168 | tf_op jit(solution)/shard_map/sub | solution.py:89
  83.3 2.0 fusion.44
  85.2 2.0 slice_subtract_fusion
  87.2 1.3 collective-permute-start.9
  88.5 1.5 slice_subtract_fusion.1
  90.2 3.7 %collective-permute-start.8 = (f32[1,8192]{1,0:T(1,128)S(1)}, f32[1,8192]{1,0:T(1,128)S(1)}, u32[]{:S(2)}, u32[]{:S(2)}) collective-permute-start(f32[1,8192]{1,0:T(1,128)S(1)} %slice_bitcast_fusion.1), channel_id=1, source_target_pairs={{2,0},{4,2},{6,4},{8,6},{10,8},{12,10},{14,12},{16,14},{18,16},{20... | collective-permute-start | bytes 98312 | tf_op jit(solution)/shard_map/ppermute | solution.py:20
  93.9 0.8 slice_subtract_fusion.9
  94.8 2.1 broadcast_select_fusion.3
  96.9 6.3 %maximum_divide_fusion = f32[8,8,8192]{2,1,0:T(8,128)S(1)} fusion(f32[8,8,8192]{2,1,0:T(8,128)} %get-tuple-element.18, f32[8,8,1]{2,1,0:T(8,128)S(1)} %bitcast.167, f32[8,8,8191]{2,1,0:T(8,128)} %fusion.44, f32[8,1,8192]{2,1,0:T(1,128)S(1)} %broadcast_select_fusion.3, f32[8,7,8192]{2,1,0:T(8,128)} %slice_subtract_fusion.1, pred[8192]{0:T(1024)(128)(4,1)S(1)} %fusion.36, ...), kind=kLoop, calls=%fused_computation.64 | loop fusion | flops 12058624 | bytes 12591104 | tf_op jit(solution)/shard_map/div | solution.py:71
  103.3 1.5 collective-permute-start.10
  104.8 1.7 fusion.30
  106.7 4.3 %collective-permute-start.11 = (f32[1,64]{1,0:T(1,128)S(1)}, f32[1,64]{1,0:T(1,128)S(1)}, u32[]{:S(2)}, u32[]{:S(2)}) collective-permute-start(f32[1,64]{1,0:T(1,128)S(1)} %bitcast.186), channel_id=1, source_target_pairs={{0,1},{2,3},{4,5},{6,7},{8,9},{10,11},{12,13},{14,15},{16,17},{18,... | collective-permute-start | bytes 776 | tf_op jit(solution)/shard_map/ppermute | solution.py:20
  112.1 10.4 %fusion = (f32[]{:T(128)}, f32[]{:T(128)}, f32[]{:T(128)}, f32[64,8192]{1,0:T(8,128)}) fusion(f32[64,8192]{1,0:T(8,128)} %get-tuple-element.20, f32[64,8192]{1,0:T(8,128)S(1)} %copy-done.1, f32[64,8192]{1,0:T(8,128)} %get-tuple-element.21, f32[64,8192]{1,0:T(8,128)} %get-tuple-element.15, f32[64,8191]{1,0:T(8,128)} %bitcast.159, f32[64,1]{1,0:T(8,128)S(1)} %copy.38, ...), kind=kLoop, calls=%fused_computation.6 | loop fusion | flops 20447232 | bytes 23076876 | tf_op jit(solution)/shard_map/reduce_sum | solution.py:85
  122.5 2.4 broadcast_in_dim.76
  124.9 3.5 %scatter_fusion = f32[16,8,8192]{2,1,0:T(8,128)} fusion(f32[16,8,8192]{2,1,0:T(8,128)} %broadcast_in_dim.76, s32[8]{0:T(128)S(1)} %fusion.38, f32[8,8,8192]{2,1,0:T(8,128)S(1)} %bitcast.160), kind=kCustom, calls=%fused_computation.2 | custom fusion | bytes 6291488 | tf_op jit(solution)/shard_map/scatter | solution.py:94
  128.5 12.3 %all-to-all-start = ((f32[16,8,8192]{2,1,0:T(8,128)}), f32[16,8,8192]{2,1,0:T(8,128)}, u32[]{:S(2)}, u32[]{:S(2)}) async-start(f32[16,8,8192]{2,1,0:T(8,128)} %scatter_fusion), calls=%async_computation | async-start | bytes 8388608 | tf_op jit(solution)/shard_map/all_to_all | solution.py:93
  140.8 2.5 sort.17
  143.3 7.9 %sqrt_reduce_fusion.2 = (f32[]{:T(128)}, f32[]{:T(128)}, f32[]{:T(128)}) fusion(f32[8,8,1]{2,1,0:T(8,128)S(1)} %bitcast.164, f32[8,8,8191]{2,1,0:T(8,128)} %fusion.46, pred[8192]{0:T(1024)(128)(4,1)S(1)} %fusion.36, f32[8,1,8192]{2,1,0:T(1,128)S(1)} %broadcast_select_fusion.5, f32[8,7,8192]{2,1,0:T(8,128)S(1)} %copy-done.5, f32[8,8,1]{2,1,0:T(8,128)S(1)} %bitcast.168, ...), kind=kLoop, calls=%fused_computation.63 | loop fusion | flops 11010045 | bytes 12591116 | tf_op jit(solution)/shard_map/reduce_sum | solution.py:85
  155.0 98.4 %all-reduce = (f32[]{:T(128)}, f32[]{:T(128)}, f32[]{:T(128)}) all-reduce(f32[]{:T(128)S(6)} %add.209, f32[]{:T(128)S(6)} %add.207, f32[]{:T(128)S(6)} %add.205), channel_id=1, replica_groups=mesh['rows'=16,'cols'=2] {'rows','cols'}, use_global_device_ids=true, to_apply=%region_10.11 | all-reduce | flops 3 | bytes 24 | tf_op jit(solution)/shard_map/psum | solution.py:88
  255.9 4.2 %gather_fusion.1 = f32[8,8,8192]{2,1,0:T(8,128)} fusion(f32[16,8,8192]{2,1,0:T(8,128)} %all-to-all-done, s32[1024]{0:T(1024)S(1)} %pad_clamp_fusion), kind=kCustom, calls=%fused_computation.1 | custom fusion | bytes 4194336 | tf_op jit(solution)/shard_map/gather | solution.py:93
  (95 shorter events, 5.4 us)
Async XLA Ops:
  1.6 14.6 %collective-permute-start = (f32[1,8192]{1,0:T(1,128)S(1)}, f32[1,8192]{1,0:T(1,128)S(1)}, u32[]{:S(2)}, u32[]{:S(2)}) collective-permute-start(f32[1,8192]{1,0:T(1,128)S(1)} %slice_bitcast_fusion.5), channel_id=1, source_target_pairs={{2,0},{4,2},{6,4},{8,6},{10,8},{12,10},{14,12},{16,14},{18,16},{20... | collective-permute-start | bytes 98312 | tf_op jit(solution)/shard_map/ppermute | solution.py:20
  5.1 11.0 %collective-permute-start.1 = (f32[1,64]{1,0:T(1,128)S(1)}, f32[1,64]{1,0:T(1,128)S(1)}, u32[]{:S(2)}, u32[]{:S(2)}) collective-permute-start(f32[1,64]{1,0:T(1,128)S(1)} %bitcast.176), channel_id=1, source_target_pairs={{1,0},{3,2},{5,4},{7,6},{9,8},{11,10},{13,12},{15,14},{17,16},{19,... | collective-permute-start | bytes 776 | tf_op jit(solution)/shard_map/ppermute | solution.py:20
  6.4 3.9 %copy-start.1 = (f32[64,8192]{1,0:T(8,128)S(1)}, f32[64,8192]{1,0:T(8,128)}, u32[]{:S(2)}) copy-start(f32[64,8192]{1,0:T(8,128)} %param.4) | copy-start | bytes 6291460
  12.3 1.9 copy-start.22
  16.7 5.3 %copy-start.4 = (f32[8,7,8192]{2,1,0:T(8,128)S(1)}, f32[8,7,8192]{2,1,0:T(8,128)}, u32[]{:S(2)}) copy-start(f32[8,7,8192]{2,1,0:T(8,128)} %slice_subtract_fusion.4) | copy-start | bytes 5505028
  16.7 5.3 %copy-start.13 = (f32[64,8191]{1,0:T(8,128)S(1)}, f32[64,8191]{1,0:T(8,128)}, u32[]{:S(2)}) copy-start(f32[64,8191]{1,0:T(8,128)} %slice_subtract_fusion.5) | copy-start | bytes 6290692
  20.7 8.4 %copy-start.12 = (f32[8,8,8192]{2,1,0:T(8,128)}, f32[8,8,8192]{2,1,0:T(8,128)S(1)}, u32[]{:S(2)}) copy-start(f32[8,8,8192]{2,1,0:T(8,128)S(1)} %fusion.34) | copy-start | bytes 6291460
  20.7 9.2 %collective-permute-start.2 = (f32[1,8192]{1,0:T(1,128)S(1)}, f32[1,8192]{1,0:T(1,128)S(1)}, u32[]{:S(2)}, u32[]{:S(2)}) collective-permute-start(f32[1,8192]{1,0:T(1,128)S(1)} %slice_bitcast_fusion.4), channel_id=1, source_target_pairs={{0,2},{2,4},{4,6},{6,8},{8,10},{10,12},{12,14},{14,16},{16,18},{18... | collective-permute-start | bytes 98312 | tf_op jit(solution)/shard_map/ppermute | solution.py:20
  23.6 1.4 copy-start.9
  25.1 4.7 %collective-permute-start.3 = (f32[1,64]{1,0:T(1,128)S(1)}, f32[1,64]{1,0:T(1,128)S(1)}, u32[]{:S(2)}, u32[]{:S(2)}) collective-permute-start(f32[1,64]{1,0:T(1,128)S(1)} %bitcast.185), channel_id=1, source_target_pairs={{0,1},{2,3},{4,5},{6,7},{8,9},{10,11},{12,13},{14,15},{16,17},{18,... | collective-permute-start | bytes 776 | tf_op jit(solution)/shard_map/ppermute | solution.py:20
  39.7 7.0 %copy-start.3 = (f32[64,8192]{1,0:T(8,128)}, f32[64,8192]{1,0:T(8,128)S(1)}, u32[]{:S(2)}) copy-start(f32[64,8192]{1,0:T(8,128)S(1)} %get-tuple-element.19) | copy-start | bytes 6291460
  43.9 7.1 %collective-permute-start.5 = (f32[1,64]{1,0:T(1,128)S(1)}, f32[1,64]{1,0:T(1,128)S(1)}, u32[]{:S(2)}, u32[]{:S(2)}) collective-permute-start(f32[1,64]{1,0:T(1,128)S(1)} %bitcast.177), channel_id=1, source_target_pairs={{1,0},{3,2},{5,4},{7,6},{9,8},{11,10},{13,12},{15,14},{17,16},{19,... | collective-permute-start | bytes 776 | tf_op jit(solution)/shard_map/ppermute | solution.py:20
  46.8 5.0 %collective-permute-start.4 = (f32[1,8192]{1,0:T(1,128)S(1)}, f32[1,8192]{1,0:T(1,128)S(1)}, u32[]{:S(2)}, u32[]{:S(2)}) collective-permute-start(f32[1,8192]{1,0:T(1,128)S(1)} %slice_bitcast_fusion.3), channel_id=1, source_target_pairs={{2,0},{4,2},{6,4},{8,6},{10,8},{12,10},{14,12},{16,14},{18,16},{20... | collective-permute-start | bytes 98312 | tf_op jit(solution)/shard_map/ppermute | solution.py:20
  53.9 9.1 %copy-start.6 = (f32[8,7,8192]{2,1,0:T(8,128)S(1)}, f32[8,7,8192]{2,1,0:T(8,128)}, u32[]{:S(2)}) copy-start(f32[8,7,8192]{2,1,0:T(8,128)} %slice_subtract_fusion.3) | copy-start | bytes 5505028
  53.9 9.1 %copy-start.10 = (f32[64,8192]{1,0:T(8,128)S(1)}, f32[64,8192]{1,0:T(8,128)}, u32[]{:S(2)}) copy-start(f32[64,8192]{1,0:T(8,128)} %copy-done.9) | copy-start | bytes 6291460
  53.9 9.1 %copy-start.15 = (f32[64,8192]{1,0:T(8,128)S(1)}, f32[64,8192]{1,0:T(8,128)}, u32[]{:S(2)}) copy-start(f32[64,8192]{1,0:T(8,128)} %get-tuple-element.22) | copy-start | bytes 6291460
  54.0 9.1 %copy-start.17 = (f32[64,8191]{1,0:T(8,128)S(1)}, f32[64,8191]{1,0:T(8,128)}, u32[]{:S(2)}) copy-start(f32[64,8191]{1,0:T(8,128)} %slice_subtract_fusion.2) | copy-start | bytes 6290692
  61.7 1.3 copy-start.18
  61.7 11.3 %collective-permute-start.6 = (f32[1,8192]{1,0:T(1,128)S(1)}, f32[1,8192]{1,0:T(1,128)S(1)}, u32[]{:S(2)}, u32[]{:S(2)}) collective-permute-start(f32[1,8192]{1,0:T(1,128)S(1)} %slice_bitcast_fusion.2), channel_id=1, source_target_pairs={{0,2},{2,4},{4,6},{6,8},{8,10},{10,12},{12,14},{14,16},{16,18},{18... | collective-permute-start | bytes 98312 | tf_op jit(solution)/shard_map/ppermute | solution.py:20
  63.1 7.5 %copy-start = (s32[128]{0:T(128)S(1)}, s32[128]{0:T(128)}, u32[]{:S(2)}) copy-start(s32[128]{0:T(128)} %param.7) | copy-start | bytes 1540
  64.8 1.3 copy-start.7
  66.3 6.6 %collective-permute-start.7 = (f32[1,64]{1,0:T(1,128)S(1)}, f32[1,64]{1,0:T(1,128)S(1)}, u32[]{:S(2)}, u32[]{:S(2)}) collective-permute-start(f32[1,64]{1,0:T(1,128)S(1)} %bitcast.182), channel_id=1, source_target_pairs={{0,1},{2,3},{4,5},{6,7},{8,9},{10,11},{12,13},{14,15},{16,17},{18,... | collective-permute-start | bytes 776 | tf_op jit(solution)/shard_map/ppermute | solution.py:20
  83.1 6.9 %copy-start.2 = (f32[64,8192]{1,0:T(8,128)}, f32[64,8192]{1,0:T(8,128)S(1)}, u32[]{:S(2)}) copy-start(f32[64,8192]{1,0:T(8,128)S(1)} %get-tuple-element.14) | copy-start | bytes 6291460
  87.2 6.6 %collective-permute-start.9 = (f32[1,64]{1,0:T(1,128)S(1)}, f32[1,64]{1,0:T(1,128)S(1)}, u32[]{:S(2)}, u32[]{:S(2)}) collective-permute-start(f32[1,64]{1,0:T(1,128)S(1)} %bitcast.178), channel_id=1, source_target_pairs={{1,0},{3,2},{5,4},{7,6},{9,8},{11,10},{13,12},{15,14},{17,16},{19,... | collective-permute-start | bytes 776 | tf_op jit(solution)/shard_map/ppermute | solution.py:20
  90.2 4.6 %collective-permute-start.8 = (f32[1,8192]{1,0:T(1,128)S(1)}, f32[1,8192]{1,0:T(1,128)S(1)}, u32[]{:S(2)}, u32[]{:S(2)}) collective-permute-start(f32[1,8192]{1,0:T(1,128)S(1)} %slice_bitcast_fusion.1), channel_id=1, source_target_pairs={{2,0},{4,2},{6,4},{8,6},{10,8},{12,10},{14,12},{16,14},{18,16},{20... | collective-permute-start | bytes 98312 | tf_op jit(solution)/shard_map/ppermute | solution.py:20
  96.9 7.9 %copy-start.8 = (f32[64,8192]{1,0:T(8,128)S(1)}, f32[64,8192]{1,0:T(8,128)}, u32[]{:S(2)}) copy-start(f32[64,8192]{1,0:T(8,128)} %copy-done.7) | copy-start | bytes 6291460
  96.9 7.9 %copy-start.11 = (f32[8,7,8192]{2,1,0:T(8,128)S(1)}, f32[8,7,8192]{2,1,0:T(8,128)}, u32[]{:S(2)}) copy-start(f32[8,7,8192]{2,1,0:T(8,128)} %slice_subtract_fusion.1) | copy-start | bytes 5505028
  96.9 7.9 %copy-start.14 = (f32[64,8192]{1,0:T(8,128)S(1)}, f32[64,8192]{1,0:T(8,128)}, u32[]{:S(2)}) copy-start(f32[64,8192]{1,0:T(8,128)} %get-tuple-element.16) | copy-start | bytes 6291460
  96.9 7.9 %copy-start.16 = (f32[64,8191]{1,0:T(8,128)S(1)}, f32[64,8191]{1,0:T(8,128)}, u32[]{:S(2)}) copy-start(f32[64,8191]{1,0:T(8,128)} %slice_subtract_fusion) | copy-start | bytes 6290692
  103.2 7.8 %copy-start.19 = (f32[8,8,8192]{2,1,0:T(8,128)}, f32[8,8,8192]{2,1,0:T(8,128)S(1)}, u32[]{:S(2)}) copy-start(f32[8,8,8192]{2,1,0:T(8,128)S(1)} %maximum_divide_fusion) | copy-start | bytes 6291460
  103.3 8.5 %collective-permute-start.10 = (f32[1,8192]{1,0:T(1,128)S(1)}, f32[1,8192]{1,0:T(1,128)S(1)}, u32[]{:S(2)}, u32[]{:S(2)}) collective-permute-start(f32[1,8192]{1,0:T(1,128)S(1)} %slice_bitcast_fusion), channel_id=1, source_target_pairs={{0,2},{2,4},{4,6},{6,8},{8,10},{10,12},{12,14},{14,16},{16,18},{18... | collective-permute-start | bytes 98312 | tf_op jit(solution)/shard_map/ppermute | solution.py:20
  106.5 4.7 %copy-start.20 = (f32[64,8192]{1,0:T(8,128)}, f32[64,8192]{1,0:T(8,128)S(1)}, u32[]{:S(2)}) copy-start(f32[64,8192]{1,0:T(8,128)S(1)} %fusion.30) | copy-start | bytes 6291460
  106.7 5.0 %collective-permute-start.11 = (f32[1,64]{1,0:T(1,128)S(1)}, f32[1,64]{1,0:T(1,128)S(1)}, u32[]{:S(2)}, u32[]{:S(2)}) collective-permute-start(f32[1,64]{1,0:T(1,128)S(1)} %bitcast.186), channel_id=1, source_target_pairs={{0,1},{2,3},{4,5},{6,7},{8,9},{10,11},{12,13},{14,15},{16,17},{18,... | collective-permute-start | bytes 776 | tf_op jit(solution)/shard_map/ppermute | solution.py:20
  122.5 2.4 copy-start.21
  128.5 14.8 %copy-start.5 = (f32[8,7,8192]{2,1,0:T(8,128)S(1)}, f32[8,7,8192]{2,1,0:T(8,128)}, u32[]{:S(2)}) copy-start(f32[8,7,8192]{2,1,0:T(8,128)} %slice_subtract_fusion.4) | copy-start | bytes 5505028
  128.5 127.4 %all-to-all-start = ((f32[16,8,8192]{2,1,0:T(8,128)}), f32[16,8,8192]{2,1,0:T(8,128)}, u32[]{:S(2)}, u32[]{:S(2)}) async-start(f32[16,8,8192]{2,1,0:T(8,128)} %scatter_fusion), calls=%async_computation | async-start | bytes 8388608 | tf_op jit(solution)/shard_map/all_to_all | solution.py:93
where the time goes:
time: 265 us; the launch traced here: 260 us
  blocking collectives  98.4 us (37%)
  other arithmetic  89.8 us (34%)
  starting transfers between devices  43 us (16%)
  local copies, waits for them, and re-layouts  20.9 us (8%)
  between operations  6.92 us (3%)
    psum x1, blocking collectives, per_device(): values.append(lax.psum(partial_sum, ('rows', 'cols')) / pixel_total)  98.4 us
    ppermute x12, starting transfers between devices, passed_along(): return lax.ppermute(block, axis, route)  30.8 us
    sub x2, other arithmetic, per_device(): extrap = 2.0 * updated - primal  19.3 us
    div x3, other arithmetic, per_device(): dual_rows = trial_rows / shrink  17.9 us
    all_to_all x1, starting transfers between devices, per_device(): lax.all_to_all(empty.at[targets].set(primal.reshape(blocks_here, BR, widt...  12.3 us
    reduce_sum x1, other arithmetic, per_device(): jnp.sum(0.5 * fidelity * misfit * misfit)  10.4 us
    reduce_sum x1, other arithmetic, per_device(): jnp.sum(jnp.sqrt(grad_r * grad_r + grad_c * grad_c))  7.91 us
    sub x3, other arithmetic, per_device(): shaped[:, 1:, :] - shaped[:, :-1, :]  6.94 us
  transfers between devices with their start and end apart: 13, of which 2 were waited for; matrix products, arithmetic and copies ran while one was open for 14% of the time, Pallas kernels for 0%

commit v1 on v0

v1 whole, which is shorter than its diff:
```python
import functools

import jax
import jax.numpy as jnp
from jax import lax
from jax.experimental import pallas as pl
from jax.experimental.pallas import tpu as pltpu
from jax.sharding import PartitionSpec as P

MESH = pl.DeviceIdType.MESH
BR = 8
TW = 128
ITERS = 3
TINY = 1.2e-38

fidelity_scale = 0.25
tau_step = 0.35
sigma_step = 0.35
tv_weight = 0.3


def kernel(
    n_rows,
    n_cols,
    pixel_total,
    weight_ref,
    pick_ref,
    sender_ref,
    image_ref,
    mask_ref,
    out_ref,
    obj_ref,
    img,
    fid,
    gain,
    prim,
    extr,
    du_r,
    du_c,
    done,
    outbox,
    inbox,
    part,
    part_in,
    total,
    total_in,
    load_sem,
    halo_send,
    halo_recv,
    a2a_send,
    a2a_recv,
    part_send,
    part_recv,
    total_send,
    total_recv,
):
    rows_here, width = image_ref.shape
    blocks = rows_here // BR
    tiles = width // TW
    ext_blocks = blocks + 2
    ext_rows = rows_here + 2 * BR
    ext_tiles = tiles + 2
    me = lax.axis_index("rows")
    my_col = lax.axis_index("cols")
    has_up, has_down = me > 0, me < n_rows - 1
    has_left, has_right = my_col > 0, my_col < n_cols - 1

    load = pltpu.make_async_copy(
        image_ref, img.at[pl.ds(BR, rows_here), pl.ds(TW, width)], load_sem
    )
    load.start()

    barrier = pltpu.get_barrier_semaphore()

    @pl.loop(1, n_rows)
    def _(k):
        pl.semaphore_signal(
            barrier, inc=1, device_id={"rows": lax.rem(me + k, n_rows)}, device_id_type=MESH
        )

    @pl.loop(1, n_cols)
    def _(k):
        pl.semaphore_signal(
            barrier, inc=1, device_id={"cols": lax.rem(my_col + k, n_cols)}, device_id_type=MESH
        )

    zero_rows = jnp.zeros((BR, TW), jnp.float32)

    def fill_fid(b, t):
        col = pl.multiple_of(t * TW, TW)
        clear = (1 - mask_ref[b * BR : (b + 1) * BR, pl.ds(col, TW)]).astype(jnp.float32)
        weight = weight_ref[b, t].astype(jnp.float32)
        fid[(b + 1) * BR : (b + 2) * BR, pl.ds(col + TW, TW)] = fidelity_scale * weight * clear

    @pl.loop(0, tiles)
    def _(t):
        fill_fid(0, t)
        fill_fid(blocks - 1, t)

    @pl.loop(1, ext_tiles - 1)
    def _(t):
        at = pl.ds(pl.multiple_of(t * TW, TW), TW)

        @pl.when(jnp.logical_not(has_up))
        def _():
            img[0:BR, at] = zero_rows
            fid[0:BR, at] = zero_rows

        @pl.when(jnp.logical_not(has_down))
        def _():
            img[ext_rows - BR : ext_rows, at] = zero_rows
            fid[ext_rows - BR : ext_rows, at] = zero_rows

    zero_cols = jnp.zeros((ext_rows, TW), jnp.float32)

    @pl.when(jnp.logical_not(has_left))
    def _():
        img[:, 0:TW] = zero_cols
        fid[:, 0:TW] = zero_cols

    @pl.when(jnp.logical_not(has_right))
    def _():
        img[:, TW + width :] = zero_cols
        fid[:, TW + width :] = zero_cols

    pl.semaphore_wait(barrier, n_rows - 1 + n_cols - 1)

    inner = pl.ds(TW, width)

    def halo(index, src, dst, target):
        return pltpu.make_async_remote_copy(
            src_ref=src,
            dst_ref=dst,
            send_sem=halo_send.at[index],
            recv_sem=halo_recv.at[index],
            device_id=target,
            device_id_type=MESH,
        )

    up, down = {"rows": lax.rem(me + n_rows - 1, n_rows)}, {"rows": lax.rem(me + 1, n_rows)}
    left = {"cols": lax.rem(my_col + n_cols - 1, n_cols)}
    right = {"cols": lax.rem(my_col + 1, n_cols)}
    to_up_img = halo(
        0, image_ref.at[pl.ds(0, BR)], img.at[pl.ds(ext_rows - BR, BR), inner], up
    )
    to_up_fid = halo(1, fid.at[pl.ds(BR, BR), inner], fid.at[pl.ds(ext_rows - BR, BR), inner], up)
    to_down_img = halo(
        2, image_ref.at[pl.ds(rows_here - BR, BR)], img.at[pl.ds(0, BR), inner], down
    )
    to_down_fid = halo(
        3, fid.at[pl.ds(rows_here, BR), inner], fid.at[pl.ds(0, BR), inner], down
    )
    first, last = pl.ds(TW, TW), pl.ds(width, TW)
    beyond = pl.ds(TW + width, TW)
    to_left_img = halo(4, img.at[:, first], img.at[:, beyond], left)
    to_left_fid = halo(5, fid.at[:, first], fid.at[:, beyond], left)
    to_right_img = halo(6, img.at[:, last], img.at[:, pl.ds(0, TW)], right)
    to_right_fid = halo(7, fid.at[:, last], fid.at[:, pl.ds(0, TW)], right)

    @pl.when(has_up)
    def _():
        to_up_img.start()
        to_up_fid.start()

    @pl.when(has_down)
    def _():
        to_down_img.start()
        to_down_fid.start()

    @pl.loop(0, tiles)
    def _(t):
        for b in range(1, blocks - 1):
            fill_fid(b, t)

    load.wait()

    @pl.when(has_up)
    def _():
        to_up_img.wait_send()
        to_up_fid.wait_send()
        to_down_img.wait_recv()
        to_down_fid.wait_recv()

    @pl.when(has_down)
    def _():
        to_down_img.wait_send()
        to_down_fid.wait_send()
        to_up_img.wait_recv()
        to_up_fid.wait_recv()

    @pl.when(has_left)
    def _():
        to_left_img.start()
        to_left_fid.start()

    @pl.when(has_right)
    def _():
        to_right_img.start()
        to_right_fid.start()

    @pl.when(has_left)
    def _():
        to_left_img.wait_send()
        to_left_fid.wait_send()
        to_right_img.wait_recv()
        to_right_fid.wait_recv()

    @pl.when(has_right)
    def _():
        to_right_img.wait_send()
        to_right_fid.wait_send()
        to_left_img.wait_recv()
        to_left_fid.wait_recv()

    sub = lax.broadcasted_iota(jnp.int32, (BR, TW), 0)
    lane = lax.broadcasted_iota(jnp.int32, (BR, TW), 1)
    last_sub, first_sub = sub == BR - 1, sub == 0
    last_lane, first_lane = lane == TW - 1, lane == 0
    end_row = jnp.logical_and(last_sub, jnp.logical_not(has_down))
    end_col = jnp.logical_and(last_lane, jnp.logical_not(has_right))
    zero = jnp.zeros((BR, TW), jnp.float32)

    def one_pass(step):
        source = img if step == 0 else extr

        def at(ref, b, t):
            return ref[b * BR : (b + 1) * BR, pl.ds(pl.multiple_of(t * TW, TW), TW)]

        def body(t, carry):
            rolled, leftward, acc = carry
            after = lax.rem(t + 1, ext_tiles)
            col = pl.ds(pl.multiple_of(t * TW, TW), TW)
            stop_here = jnp.logical_and(end_col, t == tiles)
            blank = jnp.logical_and(jnp.logical_not(has_left), t == 0)
            fields = [at(source, b, t) for b in range(ext_blocks)]
            shifted = [pltpu.roll(e, BR - 1, 0) for e in fields]
            next_rolled, next_left = [], []
            above = None
            misfits, slopes = zero, zero
            for b in range(ext_blocks):
                e = fields[b]
                coming = pltpu.roll(at(source, b, after), TW - 1, 1)
                next_rolled.append(coming)
                below = shifted[min(b + 1, ext_blocks - 1)]
                g_r = jnp.where(last_sub, below, shifted[b]) - e
                g_c = jnp.where(last_lane, coming, rolled[b]) - e
                if b == blocks:
                    g_r = jnp.where(end_row, 0.0, g_r)
                g_c = jnp.where(stop_here, 0.0, g_c)
                q_r, q_c = sigma_step * g_r, sigma_step * g_c
                if step > 0:
                    q_r = q_r + at(du_r, b, t)
                    q_c = q_c + at(du_c, b, t)
                inv = jnp.minimum(1.0, tv_weight * lax.rsqrt(q_r * q_r + q_c * q_c))
                d_r, d_c = q_r * inv, q_c * inv
                if b == 0:
                    d_r = jnp.where(has_up, d_r, 0.0)
                d_c = jnp.where(blank, 0.0, d_c)
                if step < ITERS - 1:
                    du_r[b * BR : (b + 1) * BR, col] = d_r
                    du_c[b * BR : (b + 1) * BR, col] = d_c
                turned = pltpu.roll(d_r, 1, 0)
                over = turned if b == 0 else jnp.where(first_sub, above, turned)
                above = turned
                moved = pltpu.roll(d_c, 1, 1)
                before = jnp.where(first_lane, leftward[b], moved)
                next_left.append(moved)
                own = 0 < b <= blocks
                if step == ITERS - 1 and not own:
                    continue
                div = (d_r - over) + (d_c - before)
                observed = e if step == 0 else at(img, b, t)
                old = e if step == 0 else at(prim, b, t)
                f = at(fid, b, t)
                weight = tau_step * f
                if step == 0:
                    g = 1.0 / (1.0 + weight)
                    gain[b * BR : (b + 1) * BR, col] = g
                else:
                    g = at(gain, b, t)
                new = (old + tau_step * div + weight * observed) * g
                if step == ITERS - 1:
                    done[b - 1, :, col] = new
                else:
                    prim[b * BR : (b + 1) * BR, col] = new
                    extr[b * BR : (b + 1) * BR, col] = 2.0 * new - old
                if own:
                    gap = new - observed
                    misfits = misfits + f * gap * gap
                    g2 = g_r * g_r + g_c * g_c
                    slopes = slopes + g2 * lax.rsqrt(jnp.maximum(g2, TINY))
            inside = jnp.logical_and(t >= 1, t <= tiles)
            acc = acc + jnp.where(inside, 0.5 * misfits + tv_weight * slopes, 0.0)
            return next_rolled, next_left, acc

        start = [pltpu.roll(at(source, b, 0), TW - 1, 1) for b in range(ext_blocks)]
        _, _, acc = lax.fori_loop(0, ext_tiles, body, (start, [zero] * ext_blocks, zero))
        return jnp.sum(jnp.sum(acc, axis=1, keepdims=True), axis=0, keepdims=True)

    sums = [one_pass(step) for step in range(ITERS)]
    stacked = zero
    for step in range(ITERS):
        stacked = jnp.where(sub == step, sums[step], stacked)
    part[...] = stacked

    def part_copy(k):
        return pltpu.make_async_remote_copy(
            src_ref=part,
            dst_ref=part_in.at[me],
            send_sem=part_send.at[k],
            recv_sem=part_recv.at[me],
            device_id={"rows": lax.rem(me + k, n_rows)},
            device_id_type=MESH,
        )

    def block_copy(k):
        target = lax.rem(me + k, n_rows)
        return pltpu.make_async_remote_copy(
            src_ref=outbox.at[target],
            dst_ref=inbox.at[me],
            send_sem=a2a_send.at[k],
            recv_sem=a2a_recv.at[me],
            device_id={"rows": target},
            device_id_type=MESH,
        )

    def arrival(buffer, sem, source):
        return pltpu.make_async_copy(buffer.at[source], buffer.at[source], sem.at[source])

    @pl.loop(1, n_rows)
    def _(k):
        part_copy(k).start()

    @pl.loop(1, n_rows)
    def _(k):
        target = lax.rem(me + k, n_rows)
        outbox[target] = done[pick_ref[target]][:, TW : TW + width]
        block_copy(k).start()

    inbox[me] = done[pick_ref[me]][:, TW : TW + width]
    part_in[me] = stacked

    @pl.loop(1, n_rows)
    def _(k):
        arrival(part_in, part_recv, lax.rem(me + k, n_rows)).wait()

    total_here = lax.fori_loop(0, n_rows, lambda k, s: s + part_in[k], zero)
    total[...] = total_here
    total_in[my_col] = total_here

    def total_copy(k):
        return pltpu.make_async_remote_copy(
            src_ref=total,
            dst_ref=total_in.at[my_col],
            send_sem=total_send.at[k],
            recv_sem=total_recv.at[my_col],
            device_id={"cols": lax.rem(my_col + k, n_cols)},
            device_id_type=MESH,
        )

    @pl.loop(1, n_cols)
    def _(k):
        total_copy(k).start()

    @pl.loop(1, n_cols)
    def _(k):
        arrival(total_in, total_recv, lax.rem(my_col + k, n_cols)).wait()

    everything = lax.fori_loop(0, n_cols, lambda k, s: s + total_in[k], zero)
    obj_ref[...] = everything / pixel_total

    @pl.loop(1, n_rows)
    def _(k):
        arrival(inbox, a2a_recv, lax.rem(me + k, n_rows)).wait()

    for j in range(blocks):
        out_ref[j * BR : (j + 1) * BR, :] = inbox[sender_ref[j]]

    @pl.loop(1, n_rows)
    def _(k):
        block_copy(k).wait_send()
        part_copy(k).wait_send()

    @pl.loop(1, n_cols)
    def _(k):
        total_copy(k).wait_send()


def solution(mesh):
    n_rows, n_cols = mesh.shape["rows"], mesh.shape["cols"]

    def per_device(image, cloud_mask, tile_weight, owner):
        rows_here, width = image.shape
        blocks = rows_here // BR
        own_row = lax.axis_index("rows")
        pixel_total = float(owner.shape[0] * BR * width * n_cols)
        mine = lax.dynamic_slice(owner, (own_row * blocks,), (blocks,))
        devices = jnp.arange(n_rows, dtype=jnp.int32)
        local = jnp.arange(blocks, dtype=jnp.int32)
        pick = jnp.sum(
            jnp.where(mine[None, :] == devices[:, None], local[None, :], 0), axis=1, dtype=jnp.int32
        )
        owned = owner == own_row
        rank = jnp.cumsum(owned.astype(jnp.int32)) - 1
        home = jnp.arange(owner.shape[0], dtype=jnp.int32) // blocks
        sender = jnp.sum(
            jnp.where(owned[None, :] & (rank[None, :] == local[:, None]), home[None, :], 0),
            axis=1,
            dtype=jnp.int32,
        )
        ext = (rows_here + 2 * BR, width + 2 * TW)
        small = (BR, TW)
        vmem = pl.BlockSpec(memory_space=pltpu.VMEM)
        smem = pl.BlockSpec(memory_space=pltpu.SMEM)
        f32 = jnp.float32
        dma = pltpu.SemaphoreType.DMA
        out, obj = pl.pallas_call(
            functools.partial(kernel, n_rows, n_cols, pixel_total),
            out_shape=(
                jax.ShapeDtypeStruct((rows_here, width), f32),
                jax.ShapeDtypeStruct(small, f32),
            ),
            in_specs=[smem, smem, smem, pl.BlockSpec(memory_space=pl.ANY), vmem],
            out_specs=(vmem, vmem),
            scratch_shapes=[pltpu.VMEM(ext, f32)] * 7
            + [pltpu.VMEM((blocks, BR, width + 2 * TW), f32)]
            + [pltpu.VMEM((n_rows, BR, width), f32)] * 2
            + [
                pltpu.VMEM(small, f32),
                pltpu.VMEM((n_rows,) + small, f32),
                pltpu.VMEM(small, f32),
                pltpu.VMEM((n_cols,) + small, f32),
                dma,
                dma((8,)),
                dma((8,)),
                dma((n_rows,)),
                dma((n_rows,)),
                dma((n_rows,)),
                dma((n_rows,)),
                dma((n_cols,)),
                dma((n_cols,)),
            ],
            compiler_params=pltpu.CompilerParams(
                collective_id=0, has_side_effects=True, vmem_limit_bytes=60 * 1024 * 1024
            ),
        )(tile_weight, pick, sender, image, cloud_mask)
        return out, obj[:ITERS, 0]

    in_specs = (P("rows", "cols"), P("rows", "cols"), P("rows", "cols"), P())
    out_specs = (P("rows", "cols"), P())
    return jax.shard_map(
        per_device, mesh=mesh, in_specs=in_specs, out_specs=out_specs, check_vma=False
    )
```

time: 265 us -> 255 us (0.962); the launches traced: 260 us -> 255 us
  Pallas kernels: 0 us -> 247 us
  blocking collectives: 98.4 us -> 0 us
  other arithmetic: 89.8 us -> 2.17 us
  starting transfers between devices: 43 us -> 0 us
  local copies, waits for them, and re-layouts: 20.9 us -> 5.22 us
  between operations: 6.92 us -> 0.65 us
    pallas_call x0 -> x1, Pallas kernels: none -> 247 us  [per_device(): pl.pallas_call(functools.partial(kernel, n_rows, n_cols, pixel_total), ou...]
    psum x1 -> x0, blocking collectives: 98.4 us -> none  [per_device(): values.append(lax.psum(partial_sum, ('rows', 'cols')) / pixel_total)]
    sub x11 -> x1, other arithmetic: 33.9 us -> 0.1 us  [per_device(): rank = jnp.cumsum(owned.astype(jnp.int32)) - 1]
    ppermute x12 -> x0, starting transfers between devices: 30.8 us -> none  [passed_along(): return lax.ppermute(block, axis, route)]
    div x6 -> x0, other arithmetic: 22.9 us -> none  [the longest x3 17.9 us: per_device(): dual_rows = trial_rows / shrink]
    reduce_sum x2, other arithmetic: 18.3 us -> 1.23 us  [the longest x1 0.64 us: per_device(): jnp.sum(jnp.where(owned[None, :] & (rank[None, :] == local[:, None]), hom...]
    all_to_all x1 -> x0, starting transfers between devices: 12.3 us -> none  [per_device(): lax.all_to_all(empty.at[targets].set(primal.reshape(blocks_here, BR, widt...]
    concatenate x3 -> x0, other arithmetic: 5.98 us -> none  [per_device(): jnp.concatenate([extrap[:, 1:] - extrap[:, :-1], right_edge[0][:, None] -...]
  transfers between devices with their start and end apart: 13 -> 0, of which waited for: 2 -> 0; matrix products, arithmetic and copies ran while one was open for 14% -> 0% of each run, Pallas kernels for 0% -> 0%
where the time goes in v1:
time: 255 us
  Pallas kernels  247 us (97%)
  local copies, waits for them, and re-layouts  5.22 us (2%)
    pallas_call x1, Pallas kernels, per_device(): pl.pallas_call(functools.partial(kernel, n_rows, n_cols, pixel_total), ou...  247 us

profile of v1, /device:TPU:27, one launch (start us, length us, event | category | flops | bytes accessed | tf_op | source)
XLA Modules:
  0.0 254.9 jit_solution(13041577559528783516)
XLA Ops:
  0.6 0.7 dynamic_slice.3
  1.4 0.6 select_reduce_fusion.1.pick_ref
  2.0 0.7 convert_bitcast_fusion
  2.6 0.1 copy.8
  2.7 0.2 reduce-window.8
  2.9 0.1 add_reduce_fusion
  3.0 0.6 select_reduce_fusion.sender_ref
  3.7 246.8 %shard_map.59 = (f32[64,8192]{1,0:T(8,128)}, f32[8,128]{1,0:T(8,128)}) custom-call(s32[8,64]{1,0:T(8,128)} %weight_ref.1, s32[16]{0:T(128)} %select_reduce_fusion.1.pick_ref, s32[8]{0:T(128)} %select_reduce_fusion.sender_ref, f32[64,8192]{1,0:T(8,128)} %image_ref.1, s32[64,8192]{1,0:T(8,128)} %mask_ref.1), custom_call_target="tpu_custom_call" | custom-call | tf_op jit(solution)/shard_map/pallas_call | solution.py:417
  250.5 1.3 slice_reduce_fusion
  251.8 3.1 %copy.10 = f32[64,8192]{1,0:T(8,128)} copy(f32[64,8192]{1,0:T(8,128)} %get-tuple-element.10) | data formatting | bytes 4194304
  (1 shorter events, 0.0 us)

commit v2 on v1

--- a/solution.py
+++ b/solution.py
@@ -234,16 +234,13 @@
             blank = jnp.logical_and(jnp.logical_not(has_left), t == 0)
             fields = [at(source, b, t) for b in range(ext_blocks)]
             shifted = [pltpu.roll(e, BR - 1, 0) for e in fields]
-            next_rolled, next_left = [], []
-            above = None
-            misfits, slopes = zero, zero
+            coming = [pltpu.roll(at(source, b, after), TW - 1, 1) for b in range(ext_blocks)]
+            slopes_r, slopes_c, duals_r, duals_c = [], [], [], []
             for b in range(ext_blocks):
                 e = fields[b]
-                coming = pltpu.roll(at(source, b, after), TW - 1, 1)
-                next_rolled.append(coming)
                 below = shifted[min(b + 1, ext_blocks - 1)]
                 g_r = jnp.where(last_sub, below, shifted[b]) - e
-                g_c = jnp.where(last_lane, coming, rolled[b]) - e
+                g_c = jnp.where(last_lane, coming[b], rolled[b]) - e
                 if b == blocks:
                     g_r = jnp.where(end_row, 0.0, g_r)
                 g_c = jnp.where(stop_here, 0.0, g_c)
@@ -256,39 +253,52 @@
                 if b == 0:
                     d_r = jnp.where(has_up, d_r, 0.0)
                 d_c = jnp.where(blank, 0.0, d_c)
-                if step < ITERS - 1:
-                    du_r[b * BR : (b + 1) * BR, col] = d_r
-                    du_c[b * BR : (b + 1) * BR, col] = d_c
-                turned = pltpu.roll(d_r, 1, 0)
-                over = turned if b == 0 else jnp.where(first_sub, above, turned)
-                above = turned
-                moved = pltpu.roll(d_c, 1, 1)
-                before = jnp.where(first_lane, leftward[b], moved)
-                next_left.append(moved)
+                slopes_r.append(g_r)
+                slopes_c.append(g_c)
+                duals_r.append(d_r)
+                duals_c.append(d_c)
+            turned = [pltpu.roll(d, 1, 0) for d in duals_r]
+            moved = [pltpu.roll(d, 1, 1) for d in duals_c]
+            slopes = zero
+            for b in range(1, blocks + 1):
+                g2 = slopes_r[b] * slopes_r[b] + slopes_c[b] * slopes_c[b]
+                slopes = slopes + g2 * lax.rsqrt(jnp.maximum(g2, TINY))
+            misfits = zero
+            writes = []
+            for b in range(ext_blocks):
                 own = 0 < b <= blocks
                 if step == ITERS - 1 and not own:
                     continue
-                div = (d_r - over) + (d_c - before)
-                observed = e if step == 0 else at(img, b, t)
-                old = e if step == 0 else at(prim, b, t)
+                rows = slice(b * BR, (b + 1) * BR)
+                over = turned[b] if b == 0 else jnp.where(first_sub, turned[b - 1], turned[b])
+                before = jnp.where(first_lane, leftward[b], moved[b])
+                div = (duals_r[b] - over) + (duals_c[b] - before)
+                observed = fields[b] if step == 0 else at(img, b, t)
+                old = fields[b] if step == 0 else at(prim, b, t)
                 f = at(fid, b, t)
                 weight = tau_step * f
                 if step == 0:
                     g = 1.0 / (1.0 + weight)
-                    gain[b * BR : (b + 1) * BR, col] = g
+                    writes.append((gain, rows, g))
                 else:
                     g = at(gain, b, t)
                 new = (old + tau_step * div + weight * observed) * g
                 if step == ITERS - 1:
-                    done[b - 1, :, col] = new
+                    writes.append((done, b - 1, new))
                 else:
-                    prim[b * BR : (b + 1) * BR, col] = new
-                    extr[b * BR : (b + 1) * BR, col] = 2.0 * new - old
+                    writes.append((prim, rows, new))
+                    writes.append((extr, rows, 2.0 * new - old))
+                    writes.append((du_r, rows, duals_r[b]))
+                    writes.append((du_c, rows, duals_c[b]))
                 if own:
                     gap = new - observed
                     misfits = misfits + f * gap * gap
-                    g2 = g_r * g_r + g_c * g_c
-                    slopes = slopes + g2 * lax.rsqrt(jnp.maximum(g2, TINY))
+            for ref, rows, value in writes:
+                if ref is done:
+                    ref[rows, :, col] = value
+                else:
+                    ref[rows, col] = value
+            next_rolled, next_left = coming, moved
             inside = jnp.logical_and(t >= 1, t <= tiles)
             acc = acc + jnp.where(inside, 0.5 * misfits + tv_weight * slopes, 0.0)
             return next_rolled, next_left, acc

time: 255 us -> 160 us (0.63)
  Pallas kernels: 247 us -> 152 us
    pallas_call x1, Pallas kernels: 247 us -> 152 us  [per_device(): pl.pallas_call(functools.partial(kernel, n_rows, n_cols, pixel_total), ou...]
where the time goes in v2:
time: 160 us
  Pallas kernels  152 us (95%)
  local copies, waits for them, and re-layouts  5.22 us (3%)
  other arithmetic  2.17 us (1%)
    pallas_call x1, Pallas kernels, per_device(): pl.pallas_call(functools.partial(kernel, n_rows, n_cols, pixel_total), ou...  152 us

profile of v2, /device:TPU:27, one launch (start us, length us, event | category | flops | bytes accessed | tf_op | source)
XLA Modules:
  0.0 160.2 jit_solution(12730719420023992806)
XLA Ops:
  0.6 0.7 dynamic_slice.3
  1.4 0.6 select_reduce_fusion.1.pick_ref
  2.0 0.7 convert_bitcast_fusion
  2.6 0.1 copy.8
  2.7 0.2 reduce-window.8
  2.9 0.1 add_reduce_fusion
  3.0 0.6 select_reduce_fusion.sender_ref
  3.7 152.2 %shard_map.59 = (f32[64,8192]{1,0:T(8,128)}, f32[8,128]{1,0:T(8,128)}) custom-call(s32[8,64]{1,0:T(8,128)} %weight_ref.1, s32[16]{0:T(128)} %select_reduce_fusion.1.pick_ref, s32[8]{0:T(128)} %select_reduce_fusion.sender_ref, f32[64,8192]{1,0:T(8,128)} %image_ref.1, s32[64,8192]{1,0:T(8,128)} %mask_ref.1), custom_call_target="tpu_custom_call" | custom-call | tf_op jit(solution)/shard_map/pallas_call | solution.py:427
  155.9 1.3 slice_reduce_fusion
  157.2 3.1 %copy.10 = f32[64,8192]{1,0:T(8,128)} copy(f32[64,8192]{1,0:T(8,128)} %get-tuple-element.10) | data formatting | bytes 4194304
  (1 shorter events, 0.0 us)
